TPU v7x, 16 devices: a 4x2x1 block of a 4x4x4 slice. The times are simulated.
16 devices in a mesh: dp: 2 (over y, z), tp: 8 (over x, core).
Axes of the slice: x: 4, y: 2, z: 1, core: 2. Of those that a mesh axis runs over, the one named last changes fastest.
The devices are a block of a 4x4x4 slice.
Arguments:
- x: bfloat16 [128, 12288], P('dp'), parts along dimension 0
- k_cache: bfloat16 [128, 4096, 8, 128], P('dp', None, 'tp'), parts along dimension 0
- v_cache: bfloat16 [128, 4096, 8, 128], P('dp', None, 'tp'), parts along dimension 0
- gain_a: bfloat16 [12288], replicated
- wq: bfloat16 [12288, 12288], P(None, 'tp')
- wo: bfloat16 [12288, 12288], P('tp')
- gain_m: bfloat16 [12288], replicated
- w_gate: bfloat16 [12288, 33792], P(None, 'tp')
- w_up: bfloat16 [12288, 33792], P(None, 'tp')
- w_down: bfloat16 [33792, 12288], P('tp')
Outputs:
- output: bfloat16 [128, 12288], P('dp'), parts along dimension 0
There are 2 independent parts. A program takes and returns all parts, laid end to end along the dimension named above; an argument that names none is the same for every part.
All inputs are finite; a program needn't handle non-finite values.
Results may differ from a plain program's by a relative error of at most 0.017.
Values are sent between devices in bfloat16 or wider.
A program may use at most 1.5 GiB of HBM per device.

v0:
```python
import jax
import jax.numpy as jnp
from jax import lax
from jax.sharding import PartitionSpec as P

HEAD = 128
THETA = 10000


def normed(x, gain):
    wide = x.astype(jnp.float32)
    scale = lax.rsqrt(jnp.mean(wide * wide, -1, keepdims=True) + 1e-6)
    return (wide * scale * gain.astype(jnp.float32)).astype(jnp.bfloat16)


def turned(t, place, theta):
    half = t.shape[-1] // 2
    angle = place.astype(jnp.float32)[:, None] * theta ** (-jnp.arange(half, dtype=jnp.float32) / half)
    cos, sin = jnp.cos(angle)[:, None], jnp.sin(angle)[:, None]
    a, b = t[..., :half].astype(jnp.float32), t[..., half:].astype(jnp.float32)
    return jnp.concatenate([a * cos - b * sin, b * cos + a * sin], -1).astype(jnp.bfloat16)


def matmul(a, w):
    return jnp.dot(a, w, preferred_element_type=jnp.float32).astype(jnp.bfloat16)


def einsum(form, a, b):
    return jnp.einsum(form, a.astype(jnp.float32), b.astype(jnp.float32))


def seen_by(a, wq, k_cache, v_cache, head, theta):
    batch, cache, kv_heads = k_cache.shape[:3]
    place = jnp.full((batch,), cache - 1)
    q = turned(matmul(a, wq).reshape(batch, -1, head), place, theta).reshape(batch, kv_heads, -1, head)
    scores = einsum("bgsd,bugd->bgsu", q, k_cache) * head**-0.5
    weights = jax.nn.softmax(scores, -1).astype(jnp.bfloat16)
    return einsum("bgsu,bugd->bgsd", weights, v_cache).astype(jnp.bfloat16).reshape(batch, -1)


def hidden_of(b, w_gate, w_up):
    gate = jnp.dot(b, w_gate, preferred_element_type=jnp.float32)
    up = jnp.dot(b, w_up, preferred_element_type=jnp.float32)
    return (jax.nn.silu(gate) * up).astype(jnp.bfloat16)


def solution(mesh):
    def added(t, term):
        return (t.astype(jnp.float32) + lax.psum(term.astype(jnp.bfloat16), "tp").astype(jnp.float32)).astype(jnp.bfloat16)

    def step(x, k_cache, v_cache, gain_a, wq, wo, gain_m, w_gate, w_up, w_down):
        seen = seen_by(normed(x, gain_a), wq, k_cache, v_cache, HEAD, THETA)
        h = added(x, jnp.dot(seen, wo, preferred_element_type=jnp.float32))
        return added(h, jnp.dot(hidden_of(normed(h, gain_m), w_gate, w_up), w_down, preferred_element_type=jnp.float32))

    states, cache, columns, rows_of = P("dp", None), P("dp", None, "tp", None), P(None, "tp"), P("tp", None)
    return jax.shard_map(
        step,
        mesh=mesh,
        in_specs=(states, cache, cache, P(None), columns, rows_of, P(None), columns, columns, rows_of),
        out_specs=states,
        check_vma=False,
    )
```

profile of v0, /device:TPU:113, one launch (start us, length us, event | category | flops | bytes accessed | tf_op | source)
XLA Modules:
  0.0 350.5 jit_solution(1521576924822709124)
XLA Ops:
  6.5 0.0 all-reduce.3.cloned.1.call-start
  6.6 0.7 convert_element_type.66
  7.4 1.8 fusion.11
  9.2 15.7 %convolution_convert_fusion.2 = bf16[64,1536]{1,0:T(8,128)(2,1)S(1)} fusion(bf16[12288,1536]{1,0:T(8,128)(2,1)} %param.14, bf16[64,12288]{1,0:T(8,128)(2,1)} %param.10, f32[12288]{0:T(1024)S(1)} %convert_element_type.66, f32[64]{0:T(128)S(1)} %add_rsqrt_fusion.1), kind=kOutput, calls=%fused_computation.29 | convolution fusion | flops 2419163136 | bytes 39567616 | tf_op jit(solution)/shard_map/dot_general | solution.py:25
  24.9 0.1 reshape.67
  25.0 0.2 fusion.32
  25.3 32.2 %fusion.3 = f32[64,12,4096]{2,1,0:T(8,128)} fusion(bf16[64,4096,1,128]{3,1,2,0:T(8,128)(2,1)} %param.11, bf16[64,12,64]{2,1,0:T(8,128)(2,1)S(1)} %get-tuple-element.8, bf16[64,12,64]{2,1,0:T(8,128)(2,1)S(1)} %get-tuple-element.7), kind=kOutput, calls=%fused_computation.3 | convolution fusion | flops 805699584 | bytes 79888384 | tf_op jit(solution)/shard_map/bgsd,bugd->bgsu/dot_general | solution.py:29
  57.4 18.0 %fusion.50 = (f32[64,12]{1,0:T(8,128)S(1)}, f32[64,12,4096]{2,1,0:T(8,128)}) fusion(f32[64,12,4096]{2,1,0:T(8,128)} %fusion.3), kind=kOutput, calls=%fused_computation.61 | output fusion | flops 12587007 | bytes 25168896 | tf_op jit(solution)/shard_map/sub | solution.py:37
  75.5 27.6 %fusion.22 = bf16[64,12,128]{2,1,0:T(8,128)(2,1)S(1)} fusion(bf16[64,4096,1,128]{3,1,2,0:T(8,128)(2,1)} %param.12, f32[64,12,4096]{2,1,0:T(8,128)} %get-tuple-element.10, f32[64,12]{1,0:T(8,128)S(1)} %get-tuple-element.9), kind=kOutput, calls=%fused_computation.32 | convolution fusion | flops 811696128 | bytes 79891456 | tf_op jit(solution)/shard_map/bgsu,bugd->bgsd/dot_general | solution.py:29
  103.1 0.0 copy-start.1
  103.1 0.0 copy-start
  103.1 16.6 %convolution_convert_fusion.1 = bf16[64,12288]{1,0:T(8,128)(2,1)} fusion(bf16[1536,12288]{1,0:T(8,128)(2,1)} %param.15, bf16[8,8,12,128]{3,2,1,0:T(8,128)(2,1)S(1)} %bitcast.22), kind=kOutput, calls=%fused_computation.10 | convolution fusion | flops 2416705536 | bytes 39518208 | tf_op jit(solution)/shard_map/dot_general | solution.py:53
  119.7 0.1 all-reduce.3.cloned.1.call-update
  119.7 0.2 all-reduce.5.cloned.1.call-start
  120.0 0.0 copy-done.1
  120.0 56.6 %all-reduce.3.cloned.1.call-done = bf16[64,12288]{1,0:T(8,128)(2,1)} async-done(((bf16[64,12288]{1,0:T(8,128)(2,1)}), bf16[64,12288]{1,0:T(8,128)(2,1)}) %all-reduce.3.cloned.1.call-update) | async-done | bytes 1572880 | tf_op jit(solution)/shard_map/psum | solution.py:49
  176.6 0.0 copy-done
  176.6 2.1 fusion.15
  178.7 35.7 %fusion.37 = f32[64,4224]{1,0:T(8,128)S(1)} fusion(bf16[12288,4224]{1,0:T(8,128)(2,1)} %param.17, bf16[64,12288]{1,0:T(8,128)(2,1)S(1)} %get-tuple-element.6, f32[12288]{0:T(1024)S(1)} %convert_element_type.77, f32[64]{0:T(128)S(1)} %add_rsqrt_fusion), kind=kOutput, calls=%fused_computation.47 | convolution fusion | flops 6646923264 | bytes 106512640 | tf_op jit(solution)/shard_map/dot_general | solution.py:42
  214.4 35.7 %fusion.10.clone.4 = bf16[64,4224]{1,0:T(8,128)(2,1)S(1)} fusion(bf16[12288,4224]{1,0:T(8,128)(2,1)} %param.18, f32[64,4224]{1,0:T(8,128)S(1)} %fusion.37, bf16[64,12288]{1,0:T(8,128)(2,1)S(1)} %get-tuple-element.6, f32[12288]{0:T(1024)S(1)} %convert_element_type.77, f32[64]{0:T(128)S(1)} %add_rsqrt_fusion), kind=kOutput, calls=%fused_computation.14.clone.clone.clone.1 | convolution fusion | flops 6648545280 | bytes 107053312 | tf_op jit(solution)/shard_map/dot_general | solution.py:43
  250.1 35.3 %convolution_convert_fusion = bf16[64,12288]{1,0:T(8,128)(2,1)} fusion(bf16[4224,12288]{1,0:T(8,128)(2,1)} %param.19, bf16[64,4224]{1,0:T(8,128)(2,1)S(1)} %fusion.10.clone.4), kind=kOutput, calls=%fused_computation.9 | convolution fusion | flops 6644563968 | bytes 105922560 | tf_op jit(solution)/shard_map/dot_general | solution.py:54
  285.4 0.1 all-reduce.5.cloned.1.call-update
  285.4 55.3 %all-reduce.5.cloned.1.call-done = bf16[64,12288]{1,0:T(8,128)(2,1)} async-done(((bf16[64,12288]{1,0:T(8,128)(2,1)}), bf16[64,12288]{1,0:T(8,128)(2,1)}) %all-reduce.5.cloned.1.call-update) | async-done | bytes 1572880 | tf_op jit(solution)/shard_map/psum | solution.py:49
  340.8 2.9 fusion.18
  (4 shorter events, 0.1 us)
Async XLA Ops:
  6.5 170.1 %all-reduce.3.cloned.1.call-start = ((), (), s32[]{:S(2)}) async-start(), calls=%async_computation | async-start | bytes 3145728 | tf_op jit(solution)/shard_map/psum | solution.py:49
  103.1 16.9 %copy-start.1 = (bf16[12288]{0:T(1024)(128)(2,1)S(1)}, bf16[12288]{0:T(1024)(128)(2,1)}, u32[]{:S(2)}) copy-start(bf16[12288]{0:T(1024)(128)(2,1)} %param.16) | copy-start | bytes 73732
  103.1 73.5 %copy-start = (bf16[64,12288]{1,0:T(8,128)(2,1)S(1)}, bf16[64,12288]{1,0:T(8,128)(2,1)}, u32[]{:S(2)}) copy-start(bf16[64,12288]{1,0:T(8,128)(2,1)} %param.10) | copy-start | bytes 4718596
  119.7 221.0 %all-reduce.5.cloned.1.call-start = ((), (), s32[]{:S(2)}) async-start(), calls=%async_computation.1 | async-start | bytes 3145728 | tf_op jit(solution)/shard_map/psum | solution.py:49
Sparse Core Ops, SparseCore 0:
  119.9 56.6 all-reduce.2
  285.6 55.1 all-reduce.4
where the time goes:
time: 353 us; the launch traced here: 351 us
  matrix products  199 us (56%)
  waiting for transfers between devices  112 us (32%)
  other arithmetic  25.9 us (7%)
  between operations  13.5 us (4%)
    psum x2, waiting for transfers between devices, added(): lax.psum(term.astype(jnp.bfloat16), 'tp').astype(jnp.float32)  112 us
    dot_general x2, matrix products, einsum(): return jnp.einsum(form, a.astype(jnp.float32), b.astype(jnp.float32))  59.8 us
    dot_general x1, matrix products, hidden_of(): up = jnp.dot(b, w_up, preferred_element_type=jnp.float32)  35.7 us
    dot_general x1, matrix products, hidden_of(): gate = jnp.dot(b, w_gate, preferred_element_type=jnp.float32)  35.7 us
    dot_general x1, matrix products, step(): jnp.dot(hidden_of(normed(h, gain_m), w_gate, w_up), w_down, preferred_ele...  35.3 us
    sub x1, other arithmetic, seen_by(): weights = jax.nn.softmax(scores, -1).astype(jnp.bfloat16)  18 us
    dot_general x1, matrix products, step(): h = added(x, jnp.dot(seen, wo, preferred_element_type=jnp.float32))  16.6 us
    dot_general x1, matrix products, matmul(): jnp.dot(a, w, preferred_element_type=jnp.float32).astype(jnp.bfloat16)  15.7 us
  transfers between devices with their start and end apart: 2, of which 2 were waited for; matrix products, arithmetic and copies ran while one was open for 0% of the time, Pallas kernels for 0%

commit v1 on v0

v1 whole, which is shorter than its diff:
```python
import functools

import jax
import jax.numpy as jnp
from jax import lax
from jax.experimental import pallas as pl
from jax.experimental.pallas import tpu as pltpu
from jax.sharding import PartitionSpec as P

HEAD = 128
THETA = 10000
W = 512
SLOTS = 10
RING = 8
F32, BF16 = jnp.float32, jnp.bfloat16


def dot(a, b):
    return jnp.dot(a, b, preferred_element_type=F32)


def dot_t(a, b):
    return lax.dot_general(a, b, (((1,), (1,)), ((), ())), preferred_element_type=F32)


def kernel(
    n_tp, x_hbm, k_hbm, v_hbm, ga_hbm, wq, wo, gm_hbm, wg, wu, wd, cos_hbm, sin_hbm, o_hbm,
    slot, slot_sem, xs, hs, ys, a_ref, gains, trig, in_sem, out_sem, qacc, qf, sc, of, seen, acc, hidden,
    termf, send1, land1, own, send2, land2, rs1_s, rs1_r, rs2_s, rs2_r, ag1_s, ag1_r, ag2_s, ag2_r,
):
    d_model = x_hbm.shape[2]
    rows = x_hbm.shape[1]
    batch = x_hbm.shape[0] * rows
    cache = k_hbm.shape[1]
    attn = wq.shape[1]
    heads = attn // HEAD
    hp = qf.shape[0] // batch
    ff = wd.shape[0]
    n_k = a_ref.shape[0]
    kt = a_ref.shape[2]
    chips = n_tp // 2
    n_slots = slot.shape[0]

    me = lax.axis_index("tp")
    chip, core = lax.div(me, 2), lax.rem(me, 2)
    partner = 2 * chip + 1 - core

    def peer(d):
        return 2 * lax.rem(chip + d, chips) + core

    def source(d):
        return 2 * lax.rem(chip - d + chips, chips) + core

    barrier = pltpu.get_barrier_semaphore()
    for other in [partner] + [peer(d) for d in range(1, chips)]:
        pl.semaphore_signal(barrier, inc=1, device_id={"tp": other}, device_id_type=pl.DeviceIdType.MESH)

    n_q, n_pair, n_o = n_k * (attn // W), batch // 2, d_model // (2 * W)
    full = ff // W
    n_gu, n_d = full * 2 * n_k, d_model // W
    g_q, g_a = 0, n_q
    g_o = g_a + n_pair
    g_g = g_o + n_o
    g_r = g_g + n_gu
    g_d = g_r + 2
    g_end = g_d + n_d

    def at(i, step=W):
        return pl.ds(pl.multiple_of(i * step, step), step)

    def lane(i, width=HEAD):
        return pl.ds(i * width, width)

    def start(src, dst, s):
        pltpu.make_async_copy(src, dst, slot_sem.at[s]).start()

    def put_q(i, s):
        start(wq.at[at(lax.rem(i, n_k), kt), at(lax.div(i, n_k))], slot.at[s, pl.ds(0, kt)], s)

    def put_a(i, s):
        for j in range(2):
            start(k_hbm.at[2 * i + j], slot.at[s, pl.ds(0, cache), lane(j)], s)
            start(v_hbm.at[2 * i + j], slot.at[s, pl.ds(0, cache), lane(2 + j)], s)

    def put_o(i, s):
        for j in range(2):
            start(wo.at[:, at(2 * i + j)], slot.at[s, pl.ds(j * attn, attn)], s)

    def put_g(i, s):
        n, r = lax.div(i, 2 * n_k), lax.rem(i, 2 * n_k)

        @pl.when(r < n_k)
        def _():
            start(wg.at[at(r, kt), at(n)], slot.at[s, pl.ds(0, kt)], s)

        @pl.when(r >= n_k)
        def _():
            start(wu.at[at(r - n_k, kt), at(n)], slot.at[s, pl.ds(0, kt)], s)

    def put_r(i, s):
        def piece(w, k, j):
            start(w.at[pl.ds(k * kt, kt), pl.ds(full * W, HEAD)], slot.at[s, pl.ds(0, kt), lane(j)], s)

        @pl.when(i == 0)
        def _():
            for k in range(2):
                piece(wg, k, 2 * k)
                piece(wu, k, 2 * k + 1)

        @pl.when(i == 1)
        def _():
            piece(wg, 2, 0)
            piece(wu, 2, 1)

    def put_d(i, s):
        start(wd.at[:, at(i)], slot.at[s, pl.ds(0, ff)], s)

    parts = [(g_q, g_a, put_q), (g_a, g_o, put_a), (g_o, g_g, put_o), (g_g, g_r, put_g), (g_r, g_d, put_r), (g_d, g_end, put_d)]

    def issue(g, low, high):
        for lo, hi, put in parts:
            if lo < high and low < hi:

                @pl.when((g >= lo) & (g < hi))
                def _():
                    put(g - lo, lax.rem(g, n_slots))

    def arrived(g, height, width=W):
        s = lax.rem(g, n_slots)
        part = slot.at[s, pl.ds(0, height), pl.ds(0, width)]
        pltpu.make_async_copy(part, part, slot_sem.at[s]).wait()
        return s

    inputs = [
        pltpu.make_async_copy(x_hbm, xs, in_sem.at[0]),
        pltpu.make_async_copy(ga_hbm, gains.at[0], in_sem.at[1]),
        pltpu.make_async_copy(gm_hbm, gains.at[1], in_sem.at[2]),
        pltpu.make_async_copy(cos_hbm, trig.at[0], in_sem.at[3]),
        pltpu.make_async_copy(sin_hbm, trig.at[1], in_sem.at[4]),
    ]
    for c in inputs:
        c.start()
    for g in range(n_slots):
        issue(jnp.int32(g), g, g + 1)
    for c in inputs:
        c.wait()

    def norm_into(src, gain):
        for i in range(batch // 16):
            per = 16 // rows
            wide = jnp.concatenate([src[i * per + j].astype(F32) for j in range(per)], 0)
            scale = lax.rsqrt(jnp.mean(wide * wide, -1, keepdims=True) + 1e-6)
            out = (wide * scale * gain.astype(F32)).astype(BF16)
            for k in range(n_k):
                a_ref[k, pl.ds(16 * i, 16)] = out[:, k * kt : (k + 1) * kt]

    norm_into(xs, gains[0])

    qf[...] = jnp.zeros_like(qf)

    @pl.loop(0, n_q)
    def _(i):
        s = arrived(g_q + i, kt)
        n, k = lax.div(i, n_k), lax.rem(i, n_k)
        qacc[n] = dot(a_ref[k], slot[s, pl.ds(0, kt)]) + jnp.where(k == 0, 0.0, qacc[n])
        issue(g_q + i + n_slots, g_q + n_slots, g_a + n_slots)

    for h in range(heads):
        t = qacc[h * HEAD // W, :, (h * HEAD) % W : (h * HEAD) % W + HEAD].astype(BF16).astype(F32)
        t = t * trig[0] + pltpu.roll(t, HEAD // 2, 1) * trig[1]
        qf[pl.ds(h, batch, stride=hp)] = t.astype(BF16).astype(F32)

    parts_of = 4
    step = cache // parts_of

    def queries(i):
        base = pl.multiple_of(i * 2 * hp, 2 * hp)
        q0, q1 = qf[pl.ds(base, hp)], qf[pl.ds(base + hp, hp)]
        zero = jnp.zeros((hp, HEAD), F32)
        return jnp.concatenate([jnp.concatenate([q0, zero], 1), jnp.concatenate([zero, q1], 1)], 0).astype(BF16)

    def attend(i, score, weigh):
        if score:
            s = arrived(g_a + i, cache)
            q = queries(i)
        if weigh:
            s1 = lax.rem(g_a + i - 1, n_slots)
            old = sc[lax.rem(i + 1, 2)]
            top = jnp.max(old, -1, keepdims=True)
        new, e, total, out = [], [], 0.0, 0.0
        for j in range(parts_of):
            if score:
                new.append(dot_t(q, slot[s, pl.ds(j * step, step), pl.ds(0, 2 * HEAD)]))
            if weigh:
                e.append(jnp.exp((old[:, j * step : (j + 1) * step] - top) * HEAD**-0.5))
                total = total + jnp.sum(e[-1], -1, keepdims=True)
        if weigh:
            inverse = 1.0 / total
            for j in range(parts_of):
                w = (e[j] * inverse).astype(BF16)
                out = out + dot(w, slot[s1, pl.ds(j * step, step), pl.ds(2 * HEAD, 2 * HEAD)])
        if score:
            sc[lax.rem(i, 2)] = jnp.concatenate(new, 1)
        if weigh:
            base = pl.multiple_of((i - 1) * 2 * hp, 2 * hp)
            of[pl.ds(base, hp)] = out[:hp, :HEAD]
            of[pl.ds(base + hp, hp)] = out[hp:, HEAD:]
            issue(g_a + i - 1 + n_slots, g_a + n_slots, g_o + n_slots)

    attend(jnp.int32(0), True, False)

    @pl.loop(1, n_pair)
    def _(i):
        attend(i, True, True)

    attend(jnp.int32(n_pair), False, True)
    for h in range(heads):
        seen[:, pl.ds(h * HEAD, HEAD)] = of[pl.ds(h, batch, stride=hp)].astype(BF16)

    def remote(src, dst, send, recv, device):
        return pltpu.make_async_remote_copy(
            src_ref=src, dst_ref=dst, send_sem=send, recv_sem=recv,
            device_id={"tp": device}, device_id_type=pl.DeviceIdType.MESH,
        )

    def sum_stages(base, width, residual, result):
        cols = pl.ds(0, width)

        def of_tile(t):
            return at(t, width)

        def copy_rs1(t):
            r = lax.rem(base + t, RING)
            return remote(
                send1.at[lax.rem(t, 4), 1 - core, :, :, cols], land1.at[r, :, :, cols], rs1_s.at[r], rs1_r.at[r], partner)

        def copy_rs2(t, d):
            r = lax.rem(base + t, RING)
            return remote(
                send2.at[lax.rem(t, 4), lax.rem(chip + d, chips), :, cols], land2.at[r, d - 1, :, cols],
                rs2_s.at[r, d - 1], rs2_r.at[r, d - 1], peer(d))

        def copy_ag1(t, d):
            r = lax.rem(base + t, RING)
            mine = result.at[me, :, of_tile(t)]
            return remote(mine, mine, ag1_s.at[r, d], ag1_r.at[r, d], peer(d) if d else partner)

        def copy_ag2(t, d):
            r = lax.rem(base + t, RING)
            theirs = result.at[source(d), :, of_tile(t)]
            return remote(theirs, theirs, ag2_s.at[r, d - 1], ag2_r.at[r, d - 1], partner)

        def a(t, term):
            for p in range(n_tp):
                block = term[p * rows : (p + 1) * rows]
                termf[lax.rem(t, 4), p, :, cols] = block
                send1[lax.rem(t, 4), p % 2, p // 2, :, cols] = block.astype(BF16)
            copy_rs1(t).start()

        def b(t):
            copy_rs1(t).wait()
            r, s = lax.rem(base + t, RING), lax.rem(t, 4)
            for c in range(chips):
                both = termf[s, 2 * c + core, :, cols] + land1[r, c, :, cols].astype(F32)
                send2[s, c, :, cols] = both.astype(BF16)
            own[s, :, cols] = termf[s, me, :, cols] + land1[r, chip, :, cols].astype(F32)
            for d in range(1, chips):
                copy_rs2(t, d).start()

        def c(t):
            r, s = lax.rem(base + t, RING), lax.rem(t, 4)
            total = own[s, :, cols]
            for d in range(1, chips):
                copy_rs2(t, d).wait()
                total = total + land2[r, d - 1, :, cols].astype(F32)
            result[me, :, of_tile(t)] = (residual[me, :, of_tile(t)].astype(F32) + total).astype(BF16)
            for d in range(chips):
                copy_ag1(t, d).start()

        def d_(t):
            for d in range(chips):
                copy_ag1(t, d).wait()
            for d in range(1, chips):
                copy_ag2(t, d).start()

        def e(t):
            for d in range(1, chips):
                copy_ag2(t, d).wait()

        return a, b, c, d_, e

    def sum_loop(count, lags, stages, term_of):
        a, *later = stages

        @pl.loop(0, count + lags[-1])
        def _(i):
            for lag, stage in reversed(list(zip(lags, later, strict=True))):

                @pl.when((i >= lag) & (i - lag < count))
                def _():
                    stage(i - lag)

            @pl.when(i < count)
            def _():
                a(i, term_of(i))

    pl.semaphore_wait(barrier, chips)

    def term_o(i):
        s = arrived(g_o + i, 2 * attn)
        lhs = seen[...]
        term = jnp.concatenate([dot(lhs, slot[s, pl.ds(j * attn, attn)]) for j in range(2)], 1)
        issue(g_o + i + n_slots, g_o + n_slots, g_g + n_slots)
        return term

    sum_loop(n_o, (2, 5, 8, 10), sum_stages(0, 2 * W, xs, hs), term_o)
    norm_into(hs, gains[1])

    def gated(gate, up):
        return (jax.nn.silu(gate) * up).astype(BF16)

    @pl.loop(0, n_gu)
    def _(i):
        s = arrived(g_g + i, kt)
        n, r = lax.div(i, 2 * n_k), lax.rem(i, 2 * n_k)
        which, k = lax.div(r, n_k), lax.rem(r, n_k)
        acc[which] = dot(a_ref[k], slot[s, pl.ds(0, kt)]) + jnp.where(k == 0, 0.0, acc[which])
        issue(g_g + i + n_slots, g_g + n_slots, g_r + n_slots)

        @pl.when(r == 2 * n_k - 1)
        def _():
            hidden[:, at(n)] = gated(acc[0], acc[1])

    s = arrived(jnp.int32(g_r), kt)
    both = dot(a_ref[0], slot[s, pl.ds(0, kt), pl.ds(0, 2 * HEAD)]) + dot(a_ref[1], slot[s, pl.ds(0, kt), pl.ds(2 * HEAD, 2 * HEAD)])
    issue(jnp.int32(g_r + n_slots), g_r + n_slots, g_r + n_slots + 1)
    s = arrived(jnp.int32(g_r + 1), kt, 2 * HEAD)
    both = both + dot(a_ref[2], slot[s, pl.ds(0, kt), pl.ds(0, 2 * HEAD)])
    issue(jnp.int32(g_r + 1 + n_slots), g_r + 1 + n_slots, g_r + 2 + n_slots)
    hidden[:, pl.ds(full * W, HEAD)] = gated(both[:, :HEAD], both[:, HEAD:])

    def term_d(i):
        s = arrived(g_d + i, ff)
        term = dot(hidden[...], slot[s, pl.ds(0, ff)])
        issue(g_d + i + n_slots, g_d + n_slots, g_end)
        return term

    sum_loop(n_d, (1, 3, 5, 6), sum_stages(n_o, W, hs, ys), term_d)
    out = pltpu.make_async_copy(ys, o_hbm, out_sem)
    out.start()
    out.wait()


def solution(mesh):
    n_tp = mesh.shape["tp"]

    def step(x, k_cache, v_cache, gain_a, wq, wo, gain_m, w_gate, w_up, w_down):
        batch, d_model = x.shape
        cache, attn, ff = k_cache.shape[1], wq.shape[1], w_down.shape[0]
        rows = batch // n_tp
        n_k = 3
        kt = d_model // n_k
        heads = attn // HEAD
        hp = -(-heads // 8) * 8
        chips = n_tp // 2
        assert ff % W == HEAD and d_model % (2 * W) == 0 and attn % W == 0
        half = HEAD // 2
        angle = jnp.float32(cache - 1) * THETA ** (-jnp.arange(half, dtype=F32) / half)
        cos, sin = jnp.cos(angle)[None], jnp.sin(angle)[None]
        cos2, sin2 = jnp.concatenate([cos, cos], 1), jnp.concatenate([-sin, sin], 1)
        height = max(kt, cache, 2 * attn, ff)
        dma = pltpu.SemaphoreType.DMA
        hbm = pl.BlockSpec(memory_space=pl.ANY)
        y = pl.pallas_call(
            functools.partial(kernel, n_tp),
            out_shape=jax.ShapeDtypeStruct((n_tp, rows, d_model), BF16),
            in_specs=[hbm] * 12,
            out_specs=hbm,
            scratch_shapes=[
                pltpu.VMEM((SLOTS, height, W), BF16),
                dma((SLOTS,)),
                pltpu.VMEM((n_tp, rows, d_model), BF16),
                pltpu.VMEM((n_tp, rows, d_model), BF16),
                pltpu.VMEM((n_tp, rows, d_model), BF16),
                pltpu.VMEM((n_k, batch, kt), BF16),
                pltpu.VMEM((2, 1, d_model), BF16),
                pltpu.VMEM((2, 1, HEAD), F32),
                dma((5,)),
                dma,
                pltpu.VMEM((attn // W, batch, W), F32),
                pltpu.VMEM((batch * hp, HEAD), F32),
                pltpu.VMEM((2, 2 * hp, cache), F32),
                pltpu.VMEM((batch * hp, HEAD), F32),
                pltpu.VMEM((batch, attn), BF16),
                pltpu.VMEM((2, batch, W), F32),
                pltpu.VMEM((batch, ff), BF16),
                pltpu.VMEM((4, n_tp, rows, 2 * W), F32),
                pltpu.VMEM((4, 2, chips, rows, 2 * W), BF16),
                pltpu.VMEM((RING, chips, rows, 2 * W), BF16),
                pltpu.VMEM((4, rows, 2 * W), F32),
                pltpu.VMEM((4, chips, rows, 2 * W), BF16),
                pltpu.VMEM((RING, chips - 1, rows, 2 * W), BF16),
                dma((RING,)),
                dma((RING,)),
                dma((RING, chips - 1)),
                dma((RING, chips - 1)),
                dma((RING, chips)),
                dma((RING, chips)),
                dma((RING, chips - 1)),
                dma((RING, chips - 1)),
            ],
            compiler_params=pltpu.CompilerParams(
                collective_id=0, has_side_effects=True, vmem_limit_bytes=67043328
            ),
            name="layer",
        )(
            x.reshape(n_tp, rows, d_model),
            k_cache.reshape(batch, cache, HEAD), v_cache.reshape(batch, cache, HEAD),
            gain_a[None], wq, wo, gain_m[None], w_gate, w_up, w_down, cos2, sin2,
        )
        return y.reshape(batch, d_model)

    states, cache, columns, rows_of = P("dp", None), P("dp", None, "tp", None), P(None, "tp"), P("tp", None)
    return jax.shard_map(
        step,
        mesh=mesh,
        in_specs=(states, cache, cache, P(None), columns, rows_of, P(None), columns, columns, rows_of),
        out_specs=states,
        check_vma=False,
    )
```

time: 353 us -> 202 us (0.57)
  matrix products: 199 us -> 0 us
  Pallas kernels: 0 us -> 195 us
  waiting for transfers between devices: 112 us -> 0 us
  other arithmetic: 25.9 us -> 1.34 us
  between operations: 13.5 us -> 0.02 us
  local copies, waits for them, and re-layouts: 0.16 us -> 5.41 us
    dot_general x7 -> x0, matrix products: 199 us -> none  [the longest x2 59.8 us: einsum(): return jnp.einsum(form, a.astype(jnp.float32), b.astype(jnp.float32))]
    pallas_call x0 -> x1, Pallas kernels: none -> 195 us  [step(): pl.pallas_call(functools.partial(kernel, n_tp), out_shape=jax.ShapeDtypeS...]
    psum x2 -> x0, waiting for transfers between devices: 112 us -> none  [added(): lax.psum(term.astype(jnp.bfloat16), 'tp').astype(jnp.float32)]
    sub x1 -> x0, other arithmetic: 18 us -> none  [seen_by(): weights = jax.nn.softmax(scores, -1).astype(jnp.bfloat16)]
    reduce_sum x2 -> x0, other arithmetic: 3.88 us -> none  [normed(): scale = lax.rsqrt(jnp.mean(wide * wide, -1, keepdims=True) + 1e-06)]
    convert_element_type x3 -> x0, other arithmetic: 3.66 us -> none  [the longest x1 2.91 us: added(): (t.astype(jnp.float32) + lax.psum(term.astype(jnp.bfloat16), 'tp').astype...]
  transfers between devices with their start and end apart: 2 -> 0, of which waited for: 2 -> 0; matrix products, arithmetic and copies ran while one was open for 0% -> 0% of each run, Pallas kernels for 0% -> 0%
where the time goes in v1:
time: 202 us; the launch traced here: 201 us
  Pallas kernels  195 us (97%)
  local copies, waits for them, and re-layouts  5.41 us (3%)
    pallas_call x1, Pallas kernels, step(): pl.pallas_call(functools.partial(kernel, n_tp), out_shape=jax.ShapeDtypeS...  195 us

profile of v1, /device:TPU:113, one launch (start us, length us, event | category | flops | bytes accessed | tf_op | source)
XLA Modules:
  0.0 201.3 jit_solution(2696348813113445259)
XLA Ops:
  0.0 0.1 fusion.1
  0.1 0.6 pad_maximum_fusion.cos_hbm
  0.6 0.1 fusion
  0.7 0.7 pad_maximum_fusion.1.sin_hbm
  1.3 1.4 broadcast_in_dim.8.ga_hbm
  2.7 1.4 broadcast_in_dim.9.gm_hbm
  4.1 194.6 %layer.1 = bf16[8,8,12288]{2,1,0:T(8,128)(2,1)} custom-call(bf16[8,8,12288]{2,1,0:T(8,128)(2,1)} %bitcast.5, bf16[64,4096,128]{2,1,0:T(8,128)(2,1)} %bitcast.1.k_hbm, bf16[64,4096,128]{2,1,0:T(8,128)(2,1)} %bitcast.2.v_hbm, bf16[1,12288]{1,0:T(2,128)(2,1)} %broadcast_in_dim.8.ga_hbm, bf16[12288,1536]{1,0:T(8,128)(2,1)} %wq.1, bf16[1536,12288]{1,0:T(8,128)(2,1)} %wo.1, ...), custom_call_target="tpu_custom_call" | custom-call | tf_op jit(solution)/shard_map/layer/pallas_call | solution.py:374
  198.7 2.7 %copy.12 = bf16[64,12288]{1,0:T(8,128)(2,1)} copy(bf16[64,12288]{1,0:T(8,128)(2,1)} %bitcast.4) | data formatting | bytes 3145728

commit v2 on v1

--- a/solution.py
+++ b/solution.py
@@ -2,6 +2,7 @@
 
 import jax
 import jax.numpy as jnp
+import numpy as np
 from jax import lax
 from jax.experimental import pallas as pl
 from jax.experimental.pallas import tpu as pltpu
@@ -10,8 +11,9 @@
 HEAD = 128
 THETA = 10000
 W = 512
-SLOTS = 10
-RING = 8
+SLOTS = 11
+DEPTH = 4
+RING = 12
 F32, BF16 = jnp.float32, jnp.bfloat16
 
 
@@ -24,9 +26,9 @@
 
 
 def kernel(
-    n_tp, x_hbm, k_hbm, v_hbm, ga_hbm, wq, wo, gm_hbm, wg, wu, wd, cos_hbm, sin_hbm, o_hbm,
-    slot, slot_sem, xs, hs, ys, a_ref, gains, trig, in_sem, out_sem, qacc, qf, sc, of, seen, acc, hidden,
-    termf, send1, land1, own, send2, land2, rs1_s, rs1_r, rs2_s, rs2_r, ag1_s, ag1_r, ag2_s, ag2_r,
+    n_tp, x_hbm, k_hbm, v_hbm, ga_hbm, wq, wo, gm_hbm, wg, wu, wd, cos_hbm, sin_hbm, ys,
+    slot, slot_sem, xs, hs, a_ref, gains, trig, in_sem, qacc, qf, sc, of, seen, acc, hidden,
+    termf, send1, land1, own, send2, land2, rs1_s, rs1_r, rs2_s, rs2_r, ag_s, ag1_r, ag2_r,
 ):
     d_model = x_hbm.shape[2]
     rows = x_hbm.shape[1]
@@ -140,21 +142,22 @@
     ]
     for c in inputs:
         c.start()
-    for g in range(n_slots):
+    for g in range(2):
         issue(jnp.int32(g), g, g + 1)
     for c in inputs:
         c.wait()
+    issue(jnp.int32(2), 2, 3)
 
     def norm_into(src, gain):
         for i in range(batch // 16):
             per = 16 // rows
             wide = jnp.concatenate([src[i * per + j].astype(F32) for j in range(per)], 0)
             scale = lax.rsqrt(jnp.mean(wide * wide, -1, keepdims=True) + 1e-6)
-            out = (wide * scale * gain.astype(F32)).astype(BF16)
-            for k in range(n_k):
-                a_ref[k, pl.ds(16 * i, 16)] = out[:, k * kt : (k + 1) * kt]
-
-    norm_into(xs, gains[0])
+            for c in range(d_model // HEAD):
+                out = (wide[:, c * HEAD : (c + 1) * HEAD] * scale * gain[c : c + 1]).astype(BF16)
+                a_ref[c * HEAD // kt, pl.ds(16 * i, 16), pl.ds(c * HEAD % kt, HEAD)] = out
+
+    norm_into(xs, gains[0].astype(F32))
 
     qf[...] = jnp.zeros_like(qf)
 
@@ -163,7 +166,15 @@
         s = arrived(g_q + i, kt)
         n, k = lax.div(i, n_k), lax.rem(i, n_k)
         qacc[n] = dot(a_ref[k], slot[s, pl.ds(0, kt)]) + jnp.where(k == 0, 0.0, qacc[n])
-        issue(g_q + i + n_slots, g_q + n_slots, g_a + n_slots)
+
+        @pl.when(i < n_slots - 3)
+        def _():
+            issue(2 * i + 3, 0, 2 * n_slots)
+            issue(2 * i + 4, 0, 2 * n_slots)
+
+        @pl.when(i >= n_slots - 3)
+        def _():
+            issue(i + n_slots, n_slots, g_a + n_slots)
 
     for h in range(heads):
         t = qacc[h * HEAD // W, :, (h * HEAD) % W : (h * HEAD) % W + HEAD].astype(BF16).astype(F32)
@@ -229,68 +240,61 @@
         def of_tile(t):
             return at(t, width)
 
-        def copy_rs1(t):
-            r = lax.rem(base + t, RING)
-            return remote(
-                send1.at[lax.rem(t, 4), 1 - core, :, :, cols], land1.at[r, :, :, cols], rs1_s.at[r], rs1_r.at[r], partner)
-
-        def copy_rs2(t, d):
-            r = lax.rem(base + t, RING)
-            return remote(
-                send2.at[lax.rem(t, 4), lax.rem(chip + d, chips), :, cols], land2.at[r, d - 1, :, cols],
-                rs2_s.at[r, d - 1], rs2_r.at[r, d - 1], peer(d))
-
-        def copy_ag1(t, d):
-            r = lax.rem(base + t, RING)
-            mine = result.at[me, :, of_tile(t)]
-            return remote(mine, mine, ag1_s.at[r, d], ag1_r.at[r, d], peer(d) if d else partner)
-
-        def copy_ag2(t, d):
-            r = lax.rem(base + t, RING)
-            theirs = result.at[source(d), :, of_tile(t)]
-            return remote(theirs, theirs, ag2_s.at[r, d - 1], ag2_r.at[r, d - 1], partner)
+        def ring(t):
+            return lax.rem(base + t, RING)
+
+        def landed(ref, sem):
+            pltpu.make_async_copy(ref, ref, sem).wait()
 
         def a(t, term):
+            s = lax.rem(t, 4)
             for p in range(n_tp):
                 block = term[p * rows : (p + 1) * rows]
-                termf[lax.rem(t, 4), p, :, cols] = block
-                send1[lax.rem(t, 4), p % 2, p // 2, :, cols] = block.astype(BF16)
-            copy_rs1(t).start()
+                termf[s, p, :, cols] = block
+                send1[s, p % 2, p // 2, :, cols] = block.astype(BF16)
+            remote(send1.at[s, 1 - core, :, :, cols], land1.at[ring(t), :, :, cols], rs1_s.at[s], rs1_r.at[ring(t)], partner).start()
 
         def b(t):
-            copy_rs1(t).wait()
-            r, s = lax.rem(base + t, RING), lax.rem(t, 4)
+            r, s, s2 = ring(t), lax.rem(t, 4), lax.rem(t, 8)
+            landed(send1.at[s, 0, :, :, cols], rs1_s.at[s])
+            landed(land1.at[r, :, :, cols], rs1_r.at[r])
             for c in range(chips):
                 both = termf[s, 2 * c + core, :, cols] + land1[r, c, :, cols].astype(F32)
-                send2[s, c, :, cols] = both.astype(BF16)
-            own[s, :, cols] = termf[s, me, :, cols] + land1[r, chip, :, cols].astype(F32)
+                send2[s2, c, :, cols] = both.astype(BF16)
+            own[s2, :, cols] = termf[s, me, :, cols] + land1[r, chip, :, cols].astype(F32)
             for d in range(1, chips):
-                copy_rs2(t, d).start()
+                src = send2.at[s2, lax.rem(chip + d, chips), :, cols]
+                remote(src, land2.at[r, d - 1, :, cols], rs2_s.at[s2], rs2_r.at[r], peer(d)).start()
 
         def c(t):
-            r, s = lax.rem(base + t, RING), lax.rem(t, 4)
-            total = own[s, :, cols]
+            r, s2 = ring(t), lax.rem(t, 8)
+            landed(land2.at[r, :, :, cols], rs2_s.at[s2])
+            landed(land2.at[r, :, :, cols], rs2_r.at[r])
+            total = own[s2, :, cols]
             for d in range(1, chips):
-                copy_rs2(t, d).wait()
                 total = total + land2[r, d - 1, :, cols].astype(F32)
-            result[me, :, of_tile(t)] = (residual[me, :, of_tile(t)].astype(F32) + total).astype(BF16)
+            mine = result.at[me, :, of_tile(t)]
+            mine[...] = (residual[me, :, of_tile(t)].astype(F32) + total).astype(BF16)
             for d in range(chips):
-                copy_ag1(t, d).start()
+                remote(mine, mine, ag_s.at[0], ag1_r.at[r], peer(d) if d else partner).start()
 
         def d_(t):
-            for d in range(chips):
-                copy_ag1(t, d).wait()
+            landed(result.at[pl.ds(0, chips), :, of_tile(t)], ag1_r.at[ring(t)])
             for d in range(1, chips):
-                copy_ag2(t, d).start()
+                theirs = result.at[source(d), :, of_tile(t)]
+                remote(theirs, theirs, ag_s.at[1], ag2_r.at[ring(t)], partner).start()
 
         def e(t):
-            for d in range(1, chips):
-                copy_ag2(t, d).wait()
-
-        return a, b, c, d_, e
+            landed(result.at[pl.ds(0, chips - 1), :, of_tile(t)], ag2_r.at[ring(t)])
+
+        def end():
+            landed(result.at[pl.ds(0, chips)], ag_s.at[0])
+            landed(result.at[pl.ds(0, chips - 1)], ag_s.at[1])
+
+        return a, b, c, d_, e, end
 
     def sum_loop(count, lags, stages, term_of):
-        a, *later = stages
+        a, *later, end = stages
 
         @pl.loop(0, count + lags[-1])
         def _(i):
@@ -303,6 +307,8 @@
             @pl.when(i < count)
             def _():
                 a(i, term_of(i))
+
+        end()
 
     pl.semaphore_wait(barrier, chips)
 
@@ -313,8 +319,8 @@
         issue(g_o + i + n_slots, g_o + n_slots, g_g + n_slots)
         return term
 
-    sum_loop(n_o, (2, 5, 8, 10), sum_stages(0, 2 * W, xs, hs), term_o)
-    norm_into(hs, gains[1])
+    sum_loop(n_o, (3, 10, 17, 20), sum_stages(0, 2 * W, xs, hs), term_o)
+    norm_into(hs, gains[1].astype(F32))
 
     def gated(gate, up):
         return (jax.nn.silu(gate) * up).astype(BF16)
@@ -342,13 +348,14 @@
     def term_d(i):
         s = arrived(g_d + i, ff)
         term = dot(hidden[...], slot[s, pl.ds(0, ff)])
-        issue(g_d + i + n_slots, g_d + n_slots, g_end)
+
+        @pl.when(i >= n_slots - DEPTH)
+        def _():
+            issue(g_d + i + DEPTH, g_d + n_slots, g_end)
+
         return term
 
-    sum_loop(n_d, (1, 3, 5, 6), sum_stages(n_o, W, hs, ys), term_d)
-    out = pltpu.make_async_copy(ys, o_hbm, out_sem)
-    out.start()
-    out.wait()
+    sum_loop(n_d, (2, 7, 12, 14), sum_stages(n_o, W, hs, ys), term_d)
 
 
 def solution(mesh):
@@ -365,28 +372,26 @@
         chips = n_tp // 2
         assert ff % W == HEAD and d_model % (2 * W) == 0 and attn % W == 0
         half = HEAD // 2
-        angle = jnp.float32(cache - 1) * THETA ** (-jnp.arange(half, dtype=F32) / half)
-        cos, sin = jnp.cos(angle)[None], jnp.sin(angle)[None]
-        cos2, sin2 = jnp.concatenate([cos, cos], 1), jnp.concatenate([-sin, sin], 1)
+        angle = np.float32(cache - 1) * np.float32(THETA) ** (-np.arange(half, dtype=np.float32) / np.float32(half))
+        cos, sin = np.cos(angle)[None], np.sin(angle)[None]
+        cos2, sin2 = np.concatenate([cos, cos], 1), np.concatenate([-sin, sin], 1)
         height = max(kt, cache, 2 * attn, ff)
         dma = pltpu.SemaphoreType.DMA
         hbm = pl.BlockSpec(memory_space=pl.ANY)
         y = pl.pallas_call(
             functools.partial(kernel, n_tp),
-            out_shape=jax.ShapeDtypeStruct((n_tp, rows, d_model), BF16),
+            out_shape=pltpu.VMEM((n_tp, rows, d_model), BF16),
             in_specs=[hbm] * 12,
-            out_specs=hbm,
+            out_specs=pl.BlockSpec(memory_space=pltpu.VMEM),
             scratch_shapes=[
                 pltpu.VMEM((SLOTS, height, W), BF16),
                 dma((SLOTS,)),
                 pltpu.VMEM((n_tp, rows, d_model), BF16),
                 pltpu.VMEM((n_tp, rows, d_model), BF16),
-                pltpu.VMEM((n_tp, rows, d_model), BF16),
                 pltpu.VMEM((n_k, batch, kt), BF16),
-                pltpu.VMEM((2, 1, d_model), BF16),
+                pltpu.VMEM((2, d_model // HEAD, HEAD), BF16),
                 pltpu.VMEM((2, 1, HEAD), F32),
                 dma((5,)),
-                dma,
                 pltpu.VMEM((attn // W, batch, W), F32),
                 pltpu.VMEM((batch * hp, HEAD), F32),
                 pltpu.VMEM((2, 2 * hp, cache), F32),
@@ -397,26 +402,25 @@
                 pltpu.VMEM((4, n_tp, rows, 2 * W), F32),
                 pltpu.VMEM((4, 2, chips, rows, 2 * W), BF16),
                 pltpu.VMEM((RING, chips, rows, 2 * W), BF16),
-                pltpu.VMEM((4, rows, 2 * W), F32),
-                pltpu.VMEM((4, chips, rows, 2 * W), BF16),
+                pltpu.VMEM((8, rows, 2 * W), F32),
+                pltpu.VMEM((8, chips, rows, 2 * W), BF16),
                 pltpu.VMEM((RING, chips - 1, rows, 2 * W), BF16),
+                dma((4,)),
+                dma((RING,)),
+                dma((8,)),
+                dma((RING,)),
+                dma((2,)),
                 dma((RING,)),
                 dma((RING,)),
-                dma((RING, chips - 1)),
-                dma((RING, chips - 1)),
-                dma((RING, chips)),
-                dma((RING, chips)),
-                dma((RING, chips - 1)),
-                dma((RING, chips - 1)),
             ],
             compiler_params=pltpu.CompilerParams(
-                collective_id=0, has_side_effects=True, vmem_limit_bytes=67043328
+                collective_id=0, has_side_effects=True, vmem_limit_bytes=64600000
             ),
             name="layer",
         )(
             x.reshape(n_tp, rows, d_model),
             k_cache.reshape(batch, cache, HEAD), v_cache.reshape(batch, cache, HEAD),
-            gain_a[None], wq, wo, gain_m[None], w_gate, w_up, w_down, cos2, sin2,
+            gain_a.reshape(-1, HEAD), wq, wo, gain_m.reshape(-1, HEAD), w_gate, w_up, w_down, cos2, sin2,
         )
         return y.reshape(batch, d_model)
 

time: 202 us -> 171 us (0.85)
  Pallas kernels: 195 us -> 170 us
  local copies, waits for them, and re-layouts: 5.41 us -> 1.15 us
    pallas_call x1, Pallas kernels: 195 us -> 170 us  [step(): pl.pallas_call(functools.partial(kernel, n_tp), out_shape=pltpu.VMEM((n_t...]
    broadcast_in_dim x2 -> x0, local copies, waits for them, and re-layouts: 2.76 us -> none  [the longest x1 1.38 us: step(): gain_a[None]]
where the time goes in v2:
time: 171 us
  Pallas kernels  170 us (99%)
    pallas_call x1, Pallas kernels, step(): pl.pallas_call(functools.partial(kernel, n_tp), out_shape=pltpu.VMEM((n_t...  170 us

profile of v2, /device:TPU:113, one launch (start us, length us, event | category | flops | bytes accessed | tf_op | source)
XLA Modules:
  0.0 170.8 jit_solution(8447557279941734641)
XLA Ops:
  0.0 169.7 %layer.1 = bf16[8,8,12288]{2,1,0:T(8,128)(2,1)S(1)} custom-call(bf16[8,8,12288]{2,1,0:T(8,128)(2,1)} %bitcast.7, bf16[64,4096,128]{2,1,0:T(8,128)(2,1)} %bitcast.1.k_hbm, bf16[64,4096,128]{2,1,0:T(8,128)(2,1)} %bitcast.2.v_hbm, bf16[96,128]{1,0:T(8,128)(2,1)} %bitcast.8, bf16[12288,1536]{1,0:T(8,128)(2,1)} %wq.1, bf16[1536,12288]{1,0:T(8,128)(2,1)} %wo.1, ...), custom_call_target="tpu_custom_call" | custom-call | tf_op jit(solution)/shard_map/layer/pallas_call | solution.py:381
  169.7 1.1 copy.14

commit v3 on v2

--- a/solution.py
+++ b/solution.py
@@ -13,6 +13,7 @@
 W = 512
 SLOTS = 11
 DEPTH = 4
+WHOLE = 2
 RING = 12
 F32, BF16 = jnp.float32, jnp.bfloat16
 
@@ -27,8 +28,8 @@
 
 def kernel(
     n_tp, x_hbm, k_hbm, v_hbm, ga_hbm, wq, wo, gm_hbm, wg, wu, wd, cos_hbm, sin_hbm, ys,
-    slot, slot_sem, xs, hs, a_ref, gains, trig, in_sem, qacc, qf, sc, of, seen, acc, hidden,
-    termf, send1, land1, own, send2, land2, rs1_s, rs1_r, rs2_s, rs2_r, ag_s, ag1_r, ag2_r,
+    slot, slot_sem, hs, a_ref, gains, trig, in_sem, qacc, qf, sc, seen, acc, hidden,
+    termf, send1, land1, own, send2, land2, whole, rs1_s, rs1_r, rs2_s, rs2_r, ag_s, ag1_r, ag2_r,
 ):
     d_model = x_hbm.shape[2]
     rows = x_hbm.shape[1]
@@ -134,7 +135,7 @@
         return s
 
     inputs = [
-        pltpu.make_async_copy(x_hbm, xs, in_sem.at[0]),
+        pltpu.make_async_copy(x_hbm, hs, in_sem.at[0]),
         pltpu.make_async_copy(ga_hbm, gains.at[0], in_sem.at[1]),
         pltpu.make_async_copy(gm_hbm, gains.at[1], in_sem.at[2]),
         pltpu.make_async_copy(cos_hbm, trig.at[0], in_sem.at[3]),
@@ -157,7 +158,7 @@
                 out = (wide[:, c * HEAD : (c + 1) * HEAD] * scale * gain[c : c + 1]).astype(BF16)
                 a_ref[c * HEAD // kt, pl.ds(16 * i, 16), pl.ds(c * HEAD % kt, HEAD)] = out
 
-    norm_into(xs, gains[0].astype(F32))
+    norm_into(hs, gains[0].astype(F32))
 
     qf[...] = jnp.zeros_like(qf)
 
@@ -214,8 +215,8 @@
             sc[lax.rem(i, 2)] = jnp.concatenate(new, 1)
         if weigh:
             base = pl.multiple_of((i - 1) * 2 * hp, 2 * hp)
-            of[pl.ds(base, hp)] = out[:hp, :HEAD]
-            of[pl.ds(base + hp, hp)] = out[hp:, HEAD:]
+            qf[pl.ds(base, hp)] = out[:hp, :HEAD]
+            qf[pl.ds(base + hp, hp)] = out[hp:, HEAD:]
             issue(g_a + i - 1 + n_slots, g_a + n_slots, g_o + n_slots)
 
     attend(jnp.int32(0), True, False)
@@ -226,7 +227,7 @@
 
     attend(jnp.int32(n_pair), False, True)
     for h in range(heads):
-        seen[:, pl.ds(h * HEAD, HEAD)] = of[pl.ds(h, batch, stride=hp)].astype(BF16)
+        seen[:, pl.ds(h * HEAD, HEAD)] = qf[pl.ds(h, batch, stride=hp)].astype(BF16)
 
     def remote(src, dst, send, recv, device):
         return pltpu.make_async_remote_copy(
@@ -234,8 +235,9 @@
             device_id={"tp": device}, device_id_type=pl.DeviceIdType.MESH,
         )
 
-    def sum_stages(base, width, residual, result):
+    def sum_stages(base, width, residual, result, count, last):
         cols = pl.ds(0, width)
+        early = count - last
 
         def of_tile(t):
             return at(t, width)
@@ -246,50 +248,95 @@
         def landed(ref, sem):
             pltpu.make_async_copy(ref, ref, sem).wait()
 
+        def either(t, usual, final):
+            if last:
+                pl.when(t < early)(usual)
+                pl.when(t >= early)(final)
+            else:
+                usual()
+
         def a(t, term):
             s = lax.rem(t, 4)
-            for p in range(n_tp):
-                block = term[p * rows : (p + 1) * rows]
-                termf[s, p, :, cols] = block
-                send1[s, p % 2, p // 2, :, cols] = block.astype(BF16)
-            remote(send1.at[s, 1 - core, :, :, cols], land1.at[ring(t), :, :, cols], rs1_s.at[s], rs1_r.at[ring(t)], partner).start()
+            for c in range(chips):
+                low, high = (term[(2 * c + j) * rows : (2 * c + j + 1) * rows] for j in range(2))
+                termf[s, c, :, cols] = jnp.where(core == 0, low, high)
+                send1[s, c, :, cols] = jnp.where(core == 0, high, low).astype(BF16)
+            remote(send1.at[s, :, :, cols], land1.at[ring(t), :, :, cols], rs1_s.at[s], rs1_r.at[ring(t)], partner).start()
 
         def b(t):
             r, s, s2 = ring(t), lax.rem(t, 4), lax.rem(t, 8)
-            landed(send1.at[s, 0, :, :, cols], rs1_s.at[s])
+            landed(send1.at[s, :, :, cols], rs1_s.at[s])
             landed(land1.at[r, :, :, cols], rs1_r.at[r])
             for c in range(chips):
-                both = termf[s, 2 * c + core, :, cols] + land1[r, c, :, cols].astype(F32)
+                both = termf[s, c, :, cols] + land1[r, c, :, cols].astype(F32)
                 send2[s2, c, :, cols] = both.astype(BF16)
-            own[s2, :, cols] = termf[s, me, :, cols] + land1[r, chip, :, cols].astype(F32)
-            for d in range(1, chips):
-                src = send2.at[s2, lax.rem(chip + d, chips), :, cols]
-                remote(src, land2.at[r, d - 1, :, cols], rs2_s.at[s2], rs2_r.at[r], peer(d)).start()
+
+            def usual():
+                own[s2, :, cols] = termf[s, chip, :, cols] + land1[r, chip, :, cols].astype(F32)
+                for d in range(1, chips):
+                    src = send2.at[s2, lax.rem(chip + d, chips), :, cols]
+                    remote(src, land2.at[r, d - 1, :, cols], rs2_s.at[s2], rs2_r.at[r], peer(d)).start()
+
+            def final():
+                k = t - early
+                for d in range(1, chips):
+                    remote(send2.at[s2, :, :, cols], whole.at[k, chip], rs2_s.at[s2], rs2_r.at[r], peer(d)).start()
+                whole[k, chip] = send2[s2, :, :, cols]
+
+            either(t, usual, final)
 
         def c(t):
             r, s2 = ring(t), lax.rem(t, 8)
-            landed(land2.at[r, :, :, cols], rs2_s.at[s2])
-            landed(land2.at[r, :, :, cols], rs2_r.at[r])
-            total = own[s2, :, cols]
-            for d in range(1, chips):
-                total = total + land2[r, d - 1, :, cols].astype(F32)
-            mine = result.at[me, :, of_tile(t)]
-            mine[...] = (residual[me, :, of_tile(t)].astype(F32) + total).astype(BF16)
-            for d in range(chips):
-                remote(mine, mine, ag_s.at[0], ag1_r.at[r], peer(d) if d else partner).start()
+
+            def usual():
+                landed(land2.at[r, :, :, cols], rs2_s.at[s2])
+                landed(land2.at[r, :, :, cols], rs2_r.at[r])
+                total = own[s2, :, cols]
+                for d in range(1, chips):
+                    total = total + land2[r, d - 1, :, cols].astype(F32)
+                mine = result.at[me, :, of_tile(t)]
+                mine[...] = (residual[me, :, of_tile(t)].astype(F32) + total).astype(BF16)
+                for d in range(chips):
+                    remote(mine, mine, ag_s.at[0], ag1_r.at[r], peer(d) if d else partner).start()
+
+            def final():
+                k = t - early
+                landed(whole.at[k, pl.ds(0, chips - 1)], rs2_s.at[s2])
+                landed(whole.at[k, pl.ds(0, chips - 1)], rs2_r.at[r])
+                for c in range(chips):
+                    total = whole[k, 0, c].astype(F32)
+                    for q in range(1, chips):
+                        total = total + whole[k, q, c].astype(F32)
+                    mine = result.at[2 * c + core, :, of_tile(t)]
+                    mine[...] = (residual[2 * c + core, :, of_tile(t)].astype(F32) + total).astype(BF16)
+                    remote(mine, mine, ag_s.at[2], ag2_r.at[r], partner).start()
+
+            either(t, usual, final)
 
         def d_(t):
-            landed(result.at[pl.ds(0, chips), :, of_tile(t)], ag1_r.at[ring(t)])
-            for d in range(1, chips):
-                theirs = result.at[source(d), :, of_tile(t)]
-                remote(theirs, theirs, ag_s.at[1], ag2_r.at[ring(t)], partner).start()
+            def usual():
+                landed(result.at[pl.ds(0, chips), :, of_tile(t)], ag1_r.at[ring(t)])
+                for d in range(1, chips):
+                    theirs = result.at[source(d), :, of_tile(t)]
+                    remote(theirs, theirs, ag_s.at[1], ag2_r.at[ring(t)], partner).start()
+
+            pl.when(t < early)(usual)
 
         def e(t):
-            landed(result.at[pl.ds(0, chips - 1), :, of_tile(t)], ag2_r.at[ring(t)])
+            def usual():
+                landed(result.at[pl.ds(0, chips - 1), :, of_tile(t)], ag2_r.at[ring(t)])
+
+            def final():
+                landed(result.at[pl.ds(0, chips), :, of_tile(t)], ag2_r.at[ring(t)])
+
+            either(t, usual, final)
 
         def end():
-            landed(result.at[pl.ds(0, chips)], ag_s.at[0])
-            landed(result.at[pl.ds(0, chips - 1)], ag_s.at[1])
+            done = pl.ds(0, early * width)
+            landed(result.at[pl.ds(0, chips), :, done], ag_s.at[0])
+            landed(result.at[pl.ds(0, chips - 1), :, done], ag_s.at[1])
+            if last:
+                landed(result.at[pl.ds(0, chips), :, pl.ds(0, last * width)], ag_s.at[2])
 
         return a, b, c, d_, e, end
 
@@ -319,7 +366,7 @@
         issue(g_o + i + n_slots, g_o + n_slots, g_g + n_slots)
         return term
 
-    sum_loop(n_o, (3, 10, 17, 20), sum_stages(0, 2 * W, xs, hs), term_o)
+    sum_loop(n_o, (3, 9, 15, 18), sum_stages(0, 2 * W, hs, hs, n_o, 0), term_o)
     norm_into(hs, gains[1].astype(F32))
 
     def gated(gate, up):
@@ -355,7 +402,7 @@
 
         return term
 
-    sum_loop(n_d, (2, 7, 12, 14), sum_stages(n_o, W, hs, ys), term_d)
+    sum_loop(n_d, (2, 5, 8, 10), sum_stages(n_o, W, hs, ys, n_d, WHOLE), term_d)
 
 
 def solution(mesh):
@@ -387,7 +434,6 @@
                 pltpu.VMEM((SLOTS, height, W), BF16),
                 dma((SLOTS,)),
                 pltpu.VMEM((n_tp, rows, d_model), BF16),
-                pltpu.VMEM((n_tp, rows, d_model), BF16),
                 pltpu.VMEM((n_k, batch, kt), BF16),
                 pltpu.VMEM((2, d_model // HEAD, HEAD), BF16),
                 pltpu.VMEM((2, 1, HEAD), F32),
@@ -395,26 +441,26 @@
                 pltpu.VMEM((attn // W, batch, W), F32),
                 pltpu.VMEM((batch * hp, HEAD), F32),
                 pltpu.VMEM((2, 2 * hp, cache), F32),
-                pltpu.VMEM((batch * hp, HEAD), F32),
                 pltpu.VMEM((batch, attn), BF16),
                 pltpu.VMEM((2, batch, W), F32),
                 pltpu.VMEM((batch, ff), BF16),
-                pltpu.VMEM((4, n_tp, rows, 2 * W), F32),
-                pltpu.VMEM((4, 2, chips, rows, 2 * W), BF16),
+                pltpu.VMEM((4, chips, rows, 2 * W), F32),
+                pltpu.VMEM((4, chips, rows, 2 * W), BF16),
                 pltpu.VMEM((RING, chips, rows, 2 * W), BF16),
                 pltpu.VMEM((8, rows, 2 * W), F32),
                 pltpu.VMEM((8, chips, rows, 2 * W), BF16),
                 pltpu.VMEM((RING, chips - 1, rows, 2 * W), BF16),
+                pltpu.VMEM((max(WHOLE, 1), chips, chips, rows, W), BF16),
                 dma((4,)),
                 dma((RING,)),
                 dma((8,)),
                 dma((RING,)),
-                dma((2,)),
+                dma((3,)),
                 dma((RING,)),
                 dma((RING,)),
             ],
             compiler_params=pltpu.CompilerParams(
-                collective_id=0, has_side_effects=True, vmem_limit_bytes=64600000
+                collective_id=0, has_side_effects=True, vmem_limit_bytes=65300000
             ),
             name="layer",
         )(

time: 171 us -> 169 us (0.988)
  Pallas kernels: 170 us -> 168 us
where the time goes in v3:
time: 169 us
  Pallas kernels  168 us (99%)
    pallas_call x1, Pallas kernels, step(): pl.pallas_call(functools.partial(kernel, n_tp), out_shape=pltpu.VMEM((n_t...  168 us

profile of v3, /device:TPU:113, one launch (start us, length us, event | category | flops | bytes accessed | tf_op | source)
XLA Modules:
  0.0 169.3 jit_solution(8992516194806924967)
XLA Ops:
  0.0 168.2 %layer.1 = bf16[8,8,12288]{2,1,0:T(8,128)(2,1)S(1)} custom-call(bf16[8,8,12288]{2,1,0:T(8,128)(2,1)} %bitcast.7, bf16[64,4096,128]{2,1,0:T(8,128)(2,1)} %bitcast.1.k_hbm, bf16[64,4096,128]{2,1,0:T(8,128)(2,1)} %bitcast.2.v_hbm, bf16[96,128]{1,0:T(8,128)(2,1)} %bitcast.8, bf16[12288,1536]{1,0:T(8,128)(2,1)} %wq.1, bf16[1536,12288]{1,0:T(8,128)(2,1)} %wo.1, ...), custom_call_target="tpu_custom_call" | custom-call | tf_op jit(solution)/shard_map/layer/pallas_call | solution.py:428
  168.2 1.1 copy.14
